TPU v7x, 256 devices: a 4x2x16 block of a 4x16x16 slice. The times are simulated.
256 devices in a mesh: rep: 2 (over y), tp: 32 (over z, core), sub: 4 (over x).
Axes of the slice: x: 4, y: 2, z: 16, core: 2. Of those that a mesh axis runs over, the one named last changes fastest.
The devices are a block of a 4x16x16 slice.
Arguments:
- hidden_in: bfloat16 [128, 6144], P(('rep', 'sub'), 'tp'), parts along dimension 0, may hold values from -128 to 128
- query: bfloat16 [128, 6144], P(('rep', 'sub'), 'tp'), parts along dimension 0, may hold values from -128 to 128
- key_new: bfloat16 [128, 1024], P(('rep', 'sub'), 'tp'), parts along dimension 0, may hold values from -8 to 8
- value_new: bfloat16 [128, 1024], P(('rep', 'sub'), 'tp'), parts along dimension 0, may hold values from -6 to 6
- key_cache: bfloat16 [128, 1024, 1024], P(('rep', 'sub'), 'tp'), parts along dimension 0, may hold values from -8 to 8
- value_cache: bfloat16 [128, 1024, 1024], P(('rep', 'sub'), 'tp'), parts along dimension 0, may hold values from -6 to 6
- lengths: int32 [128], P(('rep', 'sub')), parts along dimension 0, may hold values from 2 to 1024
- out_weight: bfloat16 [6144, 6144], P('sub', 'tp'), may hold values from -0.078125 to 0.078125
- norm_gain: bfloat16 [6144], P('tp'), may hold values from 0.099609375 to 1.8984375
- router_weight: bfloat16 [6144, 4], P('tp'), may hold values from -0.078125 to 0.078125
- routes: int32 [128, 2], P(('rep', 'sub')), parts along dimension 0, may hold values from 0 to 3, all different within a row; in each aligned block of 16 rows (0 to 15, 16 to 31, ...) at most 12 rows name the same one
- gate_weight: bfloat16 [4, 6144, 8192], P('sub', None, 'tp'), may hold values from -0.078125 to 0.078125
- up_weight: bfloat16 [4, 6144, 8192], P('sub', None, 'tp'), may hold values from -0.078125 to 0.078125
- down_weight: bfloat16 [4, 8192, 6144], P('sub', 'tp'), may hold values from -0.125 to 0.125
Outputs:
- layer_out: bfloat16 [128, 6144], P(('rep', 'sub'), 'tp'), parts along dimension 0
There are 2 independent parts, one for each index of `rep`. A program takes and returns all parts, laid end to end along the dimension named above; an argument that names none is the same for every part. Nothing has to cross between parts.
Inputs may be any that keep to these rules, and one draw needn't show every extreme that they name: `routes`: the two experts of a row differ; within the 16 rows of one index of sub, no expert is named by more than 12 rows, a bound that some such block reaches.
All inputs are finite; a program needn't handle non-finite values.
Results may differ from a plain program's by a relative error of at most 0.0075.
Values may be sent and summed in bfloat16 or wider, within the bound.
A program may use at most 128 MiB of HBM per device.

v0:
```python
import jax
import jax.numpy as jnp
from jax import lax
from jax.sharding import Mesh
from jax.sharding import PartitionSpec as P

D = 6144
H = 48
KVH = 8
HD = 128
E = 4
MOST = 12
TP = ("tp_0", "tp_1")


def side_by_side(arrays, axis, dim, along):
    ends, at = ([], 0)
    for a in arrays[:-1]:
        at += a.shape[along]
        ends.append(at)
    both = jnp.concatenate(arrays, axis=along)
    return tuple(jnp.split(lax.all_gather(both, axis, axis=dim, tiled=True), ends, axis=along))


def combined_by_axis(value, axes, combine):
    for axis in axes:
        pieces = jax.tree.map(lambda part: lax.all_gather(part, axis), value)
        value = jax.tree.map(lambda part: part[0], pieces)
        for k in range(1, lax.axis_size(axis)):
            value = combine(value, jax.tree.map(lambda part: part[k], pieces))
    return value


def in_order(parts, dim):
    parts = jnp.moveaxis(parts, 0, dim)
    dims = parts.shape
    return parts.reshape(*dims[:dim], dims[dim] * dims[dim + 1], *dims[dim + 2 :])


def sent_to_all(value, axis):
    count = lax.axis_size(axis)
    return lax.all_to_all(
        jnp.broadcast_to(value[None], (count, *value.shape)), axis, 0, 0, tiled=True
    )


def gathered_copies(value, axis, dim):
    return in_order(sent_to_all(value, axis), dim)


def taken_together(value, axis):
    return sent_to_all(value, axis).sum(axis=0)


def all_blocks(value, axes, order):
    parts = value
    for k in order:
        parts = lax.all_gather(parts, axes[k])
    done = order[::-1]
    back = [done.index(k) for k in range(len(axes))]
    parts = parts.transpose(*back, *range(len(axes), parts.ndim))
    return parts.reshape(-1, *value.shape)


def gather_axes(value, axes, order, dim):
    return in_order(all_blocks(value, axes, order), dim)


def in_blocks(value, dim, count):
    dims = value.shape
    parts = value.reshape(*dims[:dim], count, dims[dim] // count, *dims[dim + 1 :])
    return jnp.moveaxis(parts, dim, 0)


def summed_on_arrival(value, axis, dim):
    count = lax.axis_size(axis)
    parts = lax.all_to_all(in_blocks(value, dim, count), axis, 0, 0, tiled=True)
    return jnp.sum(parts, axis=0)


def join_softmax(first, second):
    joined = jnp.maximum(first[0], second[0])
    first_scale = jnp.exp(first[0] - joined)
    second_scale = jnp.exp(second[0] - joined)
    totals = first[1] * first_scale + second[1] * second_scale
    summed = first[2] * first_scale[..., None] + second[2] * second_scale[..., None]
    return (joined, totals, summed)


def on_device(
    hidden_in,
    query,
    key_new,
    value_new,
    key_cache,
    value_cache,
    lengths,
    out_weight,
    norm_gain,
    router_weight,
    routes,
    gate_weight,
    up_weight,
    down_weight,
):
    seq_rows = hidden_in.shape[0]
    group_size = H // KVH
    scale_factor = 1.0 / HD**0.5
    local_len = key_cache.shape[1]
    all_query, all_key, all_value = (
        lax.all_gather(query, TP, axis=1, tiled=True),
        *side_by_side((key_new, value_new), TP, 1, 0),
    )
    query_rows = all_query.reshape(seq_rows, KVH, group_size, HD)
    cached_keys = key_cache.reshape(seq_rows, local_len, KVH, HD)
    cached_values = value_cache.reshape(seq_rows, local_len, KVH, HD).astype(jnp.float32)
    scores = (
        jnp.einsum("bkgd,bpkd->bkgp", query_rows, cached_keys, preferred_element_type=jnp.float32)
        * scale_factor
    )
    positions = lax.axis_index(TP) * local_len + jnp.arange(local_len, dtype=jnp.int32)
    valid = positions[None, :] < lengths[:, None]
    scores = jnp.where(valid[:, None, None, :], scores, -jnp.inf)
    owned_part = (
        jnp.einsum(
            "zyqn,zyn->zyq",
            query_rows,
            all_key.reshape(seq_rows, KVH, HD),
            preferred_element_type=jnp.float32,
        )
        * scale_factor
    )
    local_max = jnp.maximum(jnp.max(scores, axis=-1), owned_part)
    weights = jnp.exp(scores - local_max[..., None])
    partial_total = jnp.sum(weights, axis=-1)
    local_summed = jnp.einsum("bkgp,bpkd->bkgd", weights, cached_values)
    run_max, total, summed = combined_by_axis(
        (local_max, partial_total, local_summed), TP, join_softmax
    )
    own_weight = jnp.exp(owned_part - run_max)
    total = total + own_weight
    new_values = all_value.reshape(seq_rows, KVH, 1, HD).astype(jnp.float32)
    summed = summed + own_weight[..., None] * new_values
    attn = (summed / total[..., None]).reshape(seq_rows, H * HD).astype(jnp.bfloat16)
    column_span = attn
    projected = jnp.dot(
        column_span, gathered_copies(out_weight, "sub", 0), preferred_element_type=jnp.float32
    )
    resid = hidden_in.astype(jnp.float32) + projected
    gain_full = norm_gain.astype(jnp.float32)[None, :]
    router_full = router_weight.astype(jnp.float32)
    squares = taken_together(jnp.sum(resid * resid, axis=-1), TP)
    root = jnp.sqrt(squares / D + 1e-05)
    normed = resid / root[:, None] * gain_full
    logits = taken_together(jnp.dot(normed, router_full), TP)
    normed_low = normed.astype(jnp.bfloat16)
    expert_ids = jnp.arange(E, dtype=jnp.int32)[None, :]
    first_hot = (routes[:, 0:1] == expert_ids).astype(jnp.float32)
    second_hot = (routes[:, 1:2] == expert_ids).astype(jnp.float32)
    first_logit = jnp.sum(logits * first_hot, axis=-1)
    second_logit = jnp.sum(logits * second_hot, axis=-1)
    first_weight = 1.0 / (1.0 + jnp.exp(second_logit - first_logit))
    second_weight = 1.0 / (1.0 + jnp.exp(first_logit - second_logit))
    dense = first_weight[:, None] * first_hot + second_weight[:, None] * second_hot
    gate_local = gate_weight[0]
    up_local = up_weight[0]
    down_local = down_weight[0]
    routed_mask = first_hot + second_hot
    rank = jnp.cumsum(routed_mask, axis=0) - routed_mask
    slot_ids = jnp.arange(MOST, dtype=jnp.float32)
    selector = routed_mask.T[:, None, :] * (rank.T[:, None, :] == slot_ids[None, :, None]).astype(
        jnp.float32
    )
    send_rows = jnp.einsum(
        "emb,bc->emc", selector.astype(jnp.bfloat16), normed_low, preferred_element_type=jnp.float32
    ).astype(jnp.bfloat16)
    received = lax.all_to_all(send_rows, "sub", split_axis=0, concat_axis=0, tiled=True)
    sources, slots, column_span = received.shape
    piece = gather_axes(received.reshape(sources * slots, column_span), TP, (0, 1), 1)
    gate_out = jnp.dot(piece, gate_local, preferred_element_type=jnp.float32)
    up_out = jnp.dot(piece, up_local, preferred_element_type=jnp.float32)
    inner = (jax.nn.silu(gate_out) * up_out).astype(jnp.bfloat16)
    result = jnp.dot(inner, down_local, preferred_element_type=jnp.float32)
    outputs = summed_on_arrival(result, TP, 1).reshape(sources, slots, column_span)
    returned = lax.all_to_all(outputs, "sub", split_axis=0, concat_axis=0, tiled=True)
    weighted = selector * dense.T[:, None, :]
    mixed = jnp.einsum("emb,emc->bc", weighted, returned)
    return (resid + mixed).astype(jnp.bfloat16)


def solution(mesh):
    split = Mesh(
        mesh.devices.reshape(mesh.shape["rep"], 16, 2, mesh.shape["sub"]),
        ("rep", "tp_0", "tp_1", "sub"),
    )
    return jax.shard_map(
        on_device,
        mesh=split,
        in_specs=(
            P(("rep", "sub"), TP),
            P(("rep", "sub"), TP),
            P(("rep", "sub"), TP),
            P(("rep", "sub"), TP),
            P(("rep", "sub"), TP, None),
            P(("rep", "sub"), TP, None),
            P(("rep", "sub")),
            P("sub", TP),
            P(TP),
            P(TP, None),
            P(("rep", "sub"), None),
            P("sub", None, TP),
            P("sub", None, TP),
            P("sub", TP, None),
        ),
        out_specs=P(("rep", "sub"), TP),
        check_vma=False,
    )
```

profile of v0, /device:TPU:40, one launch (start us, length us, event | category | flops | bytes accessed | tf_op | source)
XLA Modules:
  0.0 523.5 jit_solution(8818489390149967905)
XLA Ops:
  6.6 50.3 %all-gather.4 = bf16[32,192,16]{1,2,0:T(8,128)(2,1)S(1)} all-gather(bf16[1,192,16]{1,2,0:T(8,128)(2,1)} %bitcast.708), channel_id=1, replica_groups=mesh['rep'=2,'tp_0'=16,'tp_1'=2,'sub'=4] {'tp_0','tp_1'}, dimensions={0}, use_global_device_ids=true | all-gather | bytes 202752 | tf_op jit(solution)/shard_map/all_gather | solution.py:111
  57.9 1.9 reshape.1214
  61.4 27.9 %all_gather.46 = bf16[32,1024]{0,1:T(8,128)(2,1)S(1)} all-gather(bf16[32,32]{0,1:T(8,128)(2,1)S(1)} %pad_maximum_fusion), channel_id=1, replica_groups=mesh['rep'=2,'tp_0'=16,'tp_1'=2,'sub'=4] {'tp_0','tp_1'}, dimensions={1}, use_global_device_ids=true | all-gather | bytes 67584 | tf_op jit(solution)/shard_map/all_gather | solution.py:22
  92.5 2.1 fusion.172
  95.4 1.7 fusion.16
  97.9 2.7 broadcast_in_dim.20
  100.7 4.6 all-to-all-start
  105.3 45.4 %all-gather.1 = f32[256,8,6]{2,1,0:T(8,128)S(1)} all-gather(f32[16,8,6]{2,1,0:T(8,128)S(1)} %multiply_maximum_fusion), channel_id=3, replica_groups=mesh['rep'=2,'tp_0'=16,'tp_1'=2,'sub'=4] {'tp_0'}, dimensions={0}, use_global_device_ids=true | all-gather | bytes 52224 | tf_op jit(solution)/shard_map/all_gather | solution.py:27
  151.7 1.6 copy.411
  153.3 1.6 copy.413
  154.8 1.6 copy.415
  160.0 1.6 copy.410
  161.6 1.6 copy.412
  163.1 1.6 copy.414
  164.7 1.6 copy.416
  166.3 1.6 copy.418
  167.8 1.6 copy.420
  169.4 1.6 copy.422
  171.0 1.6 copy.424
  172.5 1.6 copy.425
  175.0 1.9 all_gather.52
  179.0 1.5 copy.427
  182.0 32.6 %all-gather.2 = f32[256,8,6]{2,1,0:T(8,128)S(1)} all-gather(f32[16,8,6]{2,1,0:T(8,128)S(1)} %fusion.23), channel_id=4, replica_groups=mesh['rep'=2,'tp_0'=16,'tp_1'=2,'sub'=4] {'tp_0'}, dimensions={0}, use_global_device_ids=true | all-gather | bytes 52224 | tf_op jit(solution)/shard_map/all_gather | solution.py:27
  215.6 1.6 copy.428
  217.1 1.6 copy.429
  218.7 1.6 copy.430
  220.3 1.6 copy.431
  221.8 1.6 copy.432
  223.4 1.6 copy.433
  225.0 1.6 copy.434
  226.5 1.6 copy.435
  228.1 1.6 copy.436
  229.7 1.6 copy.437
  231.2 1.6 copy.438
  232.8 1.6 copy.439
  234.3 1.6 copy.440
  235.9 1.6 copy.441
  237.5 1.6 copy.442
  239.0 1.6 copy.443
  241.8 1.9 all_gather.55
  244.3 1.5 copy.444
  247.3 1.7 fusion.77
  249.0 1.6 copy.372
  250.6 1.6 copy.373
  252.2 1.6 copy.374
  253.9 1.6 copy.394
  309.0 3.5 copy.448
  312.5 7.3 %fusion.30 = f32[1,16,8,6,128]{4,2,3,1,0:T(8,128)S(1)} fusion(f32[256,8,6,128]{3,1,2,0:T(8,128)} %all-gather.7.cloned.1.call-done, f32[16,8,6]{1,2,0:T(8,128)S(1)} %copy-done.6, f32[16,8,6]{1,2,0:T(8,128)S(1)} %copy-done.5, f32[16,8,6]{1,2,0:T(8,128)S(1)} %copy-done.4, f32[16,8,6]{1,2,0:T(8,128)S(1)} %copy.365, f32[16,8,6]{1,2,0:T(8,128)S(1)} %copy.363, ...), kind=kLoop, calls=%fused_computation.31 | loop fusion | flops 4423680 | bytes 6776832 | tf_op jit(solution)/shard_map/add | solution.py:86
  319.9 2.6 all_gather.51
  324.0 2.6 multiply_reduce_fusion
  327.2 7.8 %all-to-all-start.1 = ((f32[32,1,16]{2,1,0:T(1,128)}), f32[32,1,16]{2,1,0:T(1,128)S(1)}, u32[]{:S(2)}, u32[]{:S(2)}) async-start(f32[32,1,16]{2,1,0:T(1,128)} %broadcast_in_dim.21), calls=%async_computation.1 | async-start | bytes 32768 | tf_op jit(solution)/shard_map/all_to_all | solution.py:42
  335.0 11.8 %all-to-all-done.1 = f32[32,1,16]{2,1,0:T(1,128)S(1)} async-done(((f32[32,1,16]{2,1,0:T(1,128)}), f32[32,1,16]{2,1,0:T(1,128)S(1)}, u32[]{:S(2)}, u32[]{:S(2)}) %all-to-all-start.1) | async-done | bytes 2080 | tf_op jit(solution)/shard_map/all_to_all | solution.py:42
  347.7 4.7 all-to-all-start.2
  352.5 13.6 %all-to-all-done.2 = f32[32,16,4]{1,2,0:T(4,128)S(1)} async-done(((f32[32,16,4]{1,2,0:T(4,128)}), f32[32,16,4]{1,2,0:T(4,128)S(1)}, u32[]{:S(2)}, u32[]{:S(2)}) %all-to-all-start.2) | async-done | bytes 8224 | tf_op jit(solution)/shard_map/all_to_all | solution.py:42
  367.4 4.9 all-to-all-start.3
  372.3 4.7 copy.405
  377.8 28.9 %all_gather.56 = bf16[16,48,192]{2,1,0:T(8,128)(2,1)S(1)} all-gather(bf16[1,48,192]{2,1,0:T(8,128)(2,1)S(1)} %all_gather_reshape.3), channel_id=1, replica_groups=mesh['rep'=2,'tp_0'=16,'tp_1'=2,'sub'=4] {'tp_0'}, dimensions={0}, use_global_device_ids=true | all-gather | bytes 313344 | tf_op jit(solution)/shard_map/all_gather | solution.py:58
  406.6 2.4 all-gather.3
  410.2 2.6 reshape.1220
  412.8 2.7 fusion.2
  415.6 5.6 %convolution_bitcast_fusion = f32[32,48,192]{2,1,0:T(8,128)} fusion(bf16[32,192,256]{2,1,0:T(8,128)(2,1)} %bitcast.699, bf16[48,6144]{1,0:T(8,128)(2,1)} %reshape.1220, bf16[1,6144,256]{2,1,0:T(8,128)(2,1)S(1)} %copy-done, f32[48,256]{1,0:T(8,128)S(1)} %fusion.2), kind=kOutput, calls=%fused_computation.4 | convolution fusion | flops 302063616 | bytes 8110080 | tf_op jit(solution)/shard_map/dot_general | solution.py:183
  421.1 83.8 %all_to_all.31 = f32[32,48,192]{2,1,0:T(8,128)} all-to-all(f32[32,48,192]{2,1,0:T(8,128)} %convolution_bitcast_fusion), channel_id=1, replica_groups=mesh['rep'=2,'tp_0'=16,'tp_1'=2,'sub'=4] {'tp_0','tp_1'}, dimensions={0} | all-to-all | bytes 2359296 | tf_op jit(solution)/shard_map/all_to_all | solution.py:77
  504.9 1.5 reduce_sum.69
  506.4 9.4 %all_to_all.32 = bf16[4,12,192]{2,1,0:T(8,128)(2,1)S(1)} all-to-all(bf16[4,12,192]{2,1,0:T(8,128)(2,1)S(1)} %reshape.1221), channel_id=1, replica_groups=mesh['rep'=2,'tp_0'=16,'tp_1'=2,'sub'=4] {'sub'}, dimensions={0} | all-to-all | bytes 36864 | tf_op jit(solution)/shard_map/all_to_all | solution.py:185
  (133 shorter events, 81.6 us)
Async XLA Ops:
  6.5 409.0 %copy-start = (bf16[1,6144,256]{2,1,0:T(8,128)(2,1)S(1)}, bf16[1,6144,256]{2,1,0:T(8,128)(2,1)}, u32[]{:S(2)}) copy-start(bf16[1,6144,256]{2,1,0:T(8,128)(2,1)} %param.26) | copy-start | bytes 9437188
  6.6 84.6 %copy-start.16 = (s32[16]{0:T(128)S(1)}, s32[16]{0:T(128)}, u32[]{:S(2)}) copy-start(s32[16]{0:T(128)} %param.20) | copy-start | bytes 196
  6.6 305.9 %all-gather.7.cloned.1.call-start = ((), (), s32[]{:S(2)}) async-start(), calls=%async_computation.6 | async-start | bytes 6684672 | tf_op jit(solution)/shard_map/all_gather | solution.py:27
  92.5 2.1 copy-start.8
  94.6 0.8 copy-start.1
  100.7 208.3 %all-to-all-start = ((bf16[4,1536,192]{1,2,0:T(8,128)(2,1)}), bf16[4,1536,192]{1,2,0:T(8,128)(2,1)}, u32[]{:S(2)}, u32[]{:S(2)}) async-start(bf16[4,1536,192]{1,2,0:T(8,128)(2,1)} %broadcast_in_dim.20), calls=%async_computation | async-start | bytes 4718592 | tf_op jit(solution)/shard_map/all_to_all | solution.py:42
  182.0 58.6 %copy-start.2 = (f32[16,8,6]{0,1,2:T(8,128)S(1)}, f32[16,8,6]{0,1,2:T(8,128)}, u32[]{:S(2)}) copy-start(f32[16,8,6]{0,1,2:T(8,128)} %copy.417) | copy-start | bytes 9220
  182.0 58.6 %copy-start.3 = (f32[16,8,6]{0,1,2:T(8,128)S(1)}, f32[16,8,6]{0,1,2:T(8,128)}, u32[]{:S(2)}) copy-start(f32[16,8,6]{0,1,2:T(8,128)} %copy.415) | copy-start | bytes 9220
  308.9 3.5 copy-start.4
  308.9 3.5 copy-start.5
  309.0 3.5 copy-start.6
  309.0 3.5 copy-start.7
  312.5 10.0 %copy-start.9 = (f32[16,8,128]{2,1,0:T(8,128)S(1)}, f32[16,8,128]{2,1,0:T(8,128)}, u32[]{:S(2)}) copy-start(f32[16,8,128]{2,1,0:T(8,128)} %copy.375) | copy-start | bytes 196612
  312.5 10.0 %copy-start.10 = (f32[16,8,6]{1,2,0:T(8,128)S(1)}, f32[16,8,6]{1,2,0:T(8,128)}, u32[]{:S(2)}) copy-start(f32[16,8,6]{1,2,0:T(8,128)} %copy.372) | copy-start | bytes 9220
  312.5 10.0 %copy-start.11 = (f32[16,8,6]{1,2,0:T(8,128)S(1)}, f32[16,8,6]{1,2,0:T(8,128)}, u32[]{:S(2)}) copy-start(f32[16,8,6]{1,2,0:T(8,128)} %copy.373) | copy-start | bytes 9220
  312.5 10.0 %copy-start.12 = (f32[16,8,6]{1,2,0:T(8,128)S(1)}, f32[16,8,6]{1,2,0:T(8,128)}, u32[]{:S(2)}) copy-start(f32[16,8,6]{1,2,0:T(8,128)} %copy.374) | copy-start | bytes 9220
  312.5 10.0 %copy-start.13 = (f32[16,8,6]{1,2,0:T(8,128)S(1)}, f32[16,8,6]{1,2,0:T(8,128)}, u32[]{:S(2)}) copy-start(f32[16,8,6]{1,2,0:T(8,128)} %copy.394) | copy-start | bytes 9220
  319.8 4.1 copy-start.14
  319.9 15.2 %copy-start.18 = (bf16[192]{0:T(256)(128)(2,1)S(1)}, bf16[192]{0:T(256)(128)(2,1)}, u32[]{:S(2)}) copy-start(bf16[192]{0:T(256)(128)(2,1)} %param.22) | copy-start | bytes 1156
  319.9 27.0 %copy-start.17 = (bf16[192,4]{0,1:T(4,128)(2,1)S(1)}, bf16[192,4]{0,1:T(4,128)(2,1)}, u32[]{:S(2)}) copy-start(bf16[192,4]{0,1:T(4,128)(2,1)} %param.23) | copy-start | bytes 4612
  319.9 32.6 %copy-start.15 = (s32[16,2]{0,1:T(2,128)S(1)}, s32[16,2]{0,1:T(2,128)}, u32[]{:S(2)}) copy-start(s32[16,2]{0,1:T(2,128)} %param.24) | copy-start | bytes 388
  327.2 19.6 %all-to-all-start.1 = ((f32[32,1,16]{2,1,0:T(1,128)}), f32[32,1,16]{2,1,0:T(1,128)S(1)}, u32[]{:S(2)}, u32[]{:S(2)}) async-start(f32[32,1,16]{2,1,0:T(1,128)} %broadcast_in_dim.21), calls=%async_computation.1 | async-start | bytes 32768 | tf_op jit(solution)/shard_map/all_to_all | solution.py:42
  347.7 18.3 %all-to-all-start.2 = ((f32[32,16,4]{1,2,0:T(4,128)}), f32[32,16,4]{1,2,0:T(4,128)S(1)}, u32[]{:S(2)}, u32[]{:S(2)}) async-start(f32[32,16,4]{1,2,0:T(4,128)} %broadcast_in_dim.22), calls=%async_computation.2 | async-start | bytes 131072 | tf_op jit(solution)/shard_map/all_to_all | solution.py:42
  367.4 10.3 %all-to-all-start.3 = ((bf16[4,12,192]{2,1,0:T(8,128)(2,1)}), bf16[4,12,192]{2,1,0:T(8,128)(2,1)S(1)}, u32[]{:S(2)}, u32[]{:S(2)}) async-start(bf16[4,12,192]{2,1,0:T(8,128)(2,1)} %convolution_convert_fusion), calls=%async_computation.3 | async-start | bytes 65536 | tf_op jit(solution)/shard_map/all_to_all | solution.py:177
Sparse Core Ops, SparseCore 0:
  98.1 87.2 all-gather.6
where the time goes:
time: 529 us; the launch traced here: 523 us
  blocking collectives  287 us (54%)
  local copies, waits for them, and re-layouts  131 us (25%)
  other arithmetic  26.3 us (5%)
  waiting for transfers between devices  26.2 us (5%)
  starting transfers between devices  22 us (4%)
  matrix products  17.6 us (3%)
  between operations  13.8 us (3%)
    all_gather x5, blocking collectives, combined_by_axis(): pieces = jax.tree.map(lambda part: lax.all_gather(part, axis), value)  84.3 us
    all_to_all x1, blocking collectives, summed_on_arrival(): parts = lax.all_to_all(in_blocks(value, dim, count), axis, 0, 0, tiled=True)  83.8 us
    unnamed x78, local copies, waits for them, and re-layouts  61.3 us
    all_gather x1, blocking collectives, on_device(): lax.all_gather(query, TP, axis=1, tiled=True)  50.3 us
    all_gather x2, blocking collectives, all_blocks(): parts = lax.all_gather(parts, axes[k])  31.2 us
    all_gather x1, blocking collectives, side_by_side(): lax.all_gather(both, axis, axis=dim, tiled=True)  27.9 us
    all_to_all x3, waiting for transfers between devices, sent_to_all(): lax.all_to_all(jnp.broadcast_to(value[None], (count, *value.shape)), axis...  25.3 us
    exp x16, local copies, waits for them, and re-layouts, join_softmax(): first_scale = jnp.exp(first[0] - joined)  22.7 us
  transfers between devices with their start and end apart: 5, of which 3 were waited for; matrix products, arithmetic and copies ran while one was open for 25% of the time, Pallas kernels for 0%

commit v1 on v0

--- a/solution.py
+++ b/solution.py
@@ -11,6 +11,11 @@
 E = 4
 MOST = 12
 TP = ("tp_0", "tp_1")
+
+
+def exchange_gather(shard, axis, dim):
+    sent = jnp.stack([shard] * lax.axis_size(axis))
+    return jnp.concatenate(lax.all_to_all(sent, axis, 0, 0), axis=dim)
 
 
 def side_by_side(arrays, axis, dim, along):
@@ -108,7 +113,7 @@
     scale_factor = 1.0 / HD**0.5
     local_len = key_cache.shape[1]
     all_query, all_key, all_value = (
-        lax.all_gather(query, TP, axis=1, tiled=True),
+        exchange_gather(query, TP, 1),
         *side_by_side((key_new, value_new), TP, 1, 0),
     )
     query_rows = all_query.reshape(seq_rows, KVH, group_size, HD)

time: 529 us -> 499 us (0.943)
  blocking collectives: 287 us -> 251 us
  starting transfers between devices: 22 us -> 49.5 us
  local copies, waits for them, and re-layouts: 131 us -> 117 us
  other arithmetic: 26.3 us -> 20.1 us
    all_gather x1 -> x0, blocking collectives: 50.3 us -> none  [on_device(): lax.all_gather(query, TP, axis=1, tiled=True)]
    all_to_all x0 -> x1, starting transfers between devices: none -> 24.7 us  [exchange_gather(): return jnp.concatenate(lax.all_to_all(sent, axis, 0, 0), axis=dim)]
    unnamed x78 -> x69, local copies, waits for them, and re-layouts: 61.3 us -> 51.3 us
    all_gather x1, blocking collectives: 27.9 us -> 36.8 us  [side_by_side(): lax.all_gather(both, axis, axis=dim, tiled=True)]
    exp x8, other arithmetic: 11.3 us -> 4.65 us  [join_softmax(): first_scale = jnp.exp(first[0] - joined)]
  transfers between devices with their start and end apart: 5 -> 6, of which waited for: 3 -> 3; matrix products, arithmetic and copies ran while one was open for 25% -> 23% of each run, Pallas kernels for 0% -> 0%
where the time goes in v1:
time: 499 us; the launch traced here: 494 us
  blocking collectives  251 us (50%)
  local copies, waits for them, and re-layouts  117 us (23%)
  starting transfers between devices  49.5 us (10%)
  waiting for transfers between devices  26.2 us (5%)
  other arithmetic  20.1 us (4%)
  matrix products  16.6 us (3%)
  between operations  13.8 us (3%)
    all_gather x5, blocking collectives, combined_by_axis(): pieces = jax.tree.map(lambda part: lax.all_gather(part, axis), value)  89.5 us
    all_to_all x1, blocking collectives, summed_on_arrival(): parts = lax.all_to_all(in_blocks(value, dim, count), axis, 0, 0, tiled=True)  83.8 us
    unnamed x69, local copies, waits for them, and re-layouts  51.3 us
    all_gather x1, blocking collectives, side_by_side(): lax.all_gather(both, axis, axis=dim, tiled=True)  36.8 us
    all_gather x2, blocking collectives, all_blocks(): parts = lax.all_gather(parts, axes[k])  31.3 us
    all_to_all x3, waiting for transfers between devices, sent_to_all(): lax.all_to_all(jnp.broadcast_to(value[None], (count, *value.shape)), axis...  25.3 us
    all_to_all x1, starting transfers between devices, exchange_gather(): return jnp.concatenate(lax.all_to_all(sent, axis, 0, 0), axis=dim)  24.7 us
    exp x16, local copies, waits for them, and re-layouts, join_softmax(): first_scale = jnp.exp(first[0] - joined)  20.6 us
  transfers between devices with their start and end apart: 6, of which 3 were waited for; matrix products, arithmetic and copies ran while one was open for 23% of the time, Pallas kernels for 0%

profile of v1, /device:TPU:40, one launch (start us, length us, event | category | flops | bytes accessed | tf_op | source)
XLA Modules:
  0.0 493.8 jit_solution(3439003489643038062)
XLA Ops:
  6.6 1.6 stack.2
  8.1 24.7 %all-to-all-start = ((bf16[32,16,192]{2,1,0:T(8,128)(2,1)}), bf16[32,16,192]{2,1,0:T(8,128)(2,1)S(1)}, u32[]{:S(2)}, u32[]{:S(2)}) async-start(bf16[32,16,192]{2,1,0:T(8,128)(2,1)} %stack.2), calls=%async_computation | async-start | bytes 524288 | tf_op jit(solution)/shard_map/all_to_all | solution.py:18
  34.6 36.8 %all_gather.42 = bf16[32,1024]{0,1:T(8,128)(2,1)S(1)} all-gather(bf16[32,32]{0,1:T(8,128)(2,1)S(1)} %pad_maximum_fusion), channel_id=1, replica_groups=mesh['rep'=2,'tp_0'=16,'tp_1'=2,'sub'=4] {'tp_0','tp_1'}, dimensions={1}, use_global_device_ids=true | all-gather | bytes 67584 | tf_op jit(solution)/shard_map/all_gather | solution.py:27
  76.5 2.0 fusion.172
  79.3 1.7 fusion.16
  81.9 2.8 broadcast_in_dim.20
  84.6 4.6 all-to-all-start.1
  90.0 42.5 %all-gather.1 = f32[256,8,6]{2,1,0:T(8,128)S(1)} all-gather(f32[16,8,6]{2,1,0:T(8,128)S(1)} %multiply_maximum_fusion), channel_id=3, replica_groups=mesh['rep'=2,'tp_0'=16,'tp_1'=2,'sub'=4] {'tp_0'}, dimensions={0}, use_global_device_ids=true | all-gather | bytes 52224 | tf_op jit(solution)/shard_map/all_gather | solution.py:32
  138.5 1.6 copy.409
  140.1 1.6 copy.411
  147.5 1.9 all_gather.48
  150.1 1.5 copy.425
  151.5 1.5 copy.426
  154.5 40.8 %all-gather.2 = f32[256,8,6]{2,1,0:T(8,128)S(1)} all-gather(f32[16,8,6]{2,1,0:T(8,128)S(1)} %fusion.23), channel_id=4, replica_groups=mesh['rep'=2,'tp_0'=16,'tp_1'=2,'sub'=4] {'tp_0'}, dimensions={0}, use_global_device_ids=true | all-gather | bytes 52224 | tf_op jit(solution)/shard_map/all_gather | solution.py:32
  196.4 1.6 copy.427
  197.9 1.6 copy.428
  199.5 1.6 copy.429
  201.1 1.6 copy.430
  202.6 1.6 copy.431
  204.2 1.6 copy.432
  205.8 1.6 copy.433
  207.3 1.6 copy.434
  208.9 1.6 copy.435
  210.5 1.6 copy.436
  212.0 1.6 copy.437
  213.6 1.6 copy.438
  215.1 1.6 copy.439
  216.7 1.6 copy.440
  218.3 1.6 copy.441
  219.8 1.6 copy.442
  222.5 1.9 all_gather.51
  225.0 1.5 copy.443
  226.5 1.5 copy.444
  228.0 1.7 fusion.77
  229.7 1.6 copy.371
  231.3 1.6 copy.372
  232.9 1.6 copy.373
  234.6 1.6 copy.393
  246.5 1.5 copy.350
  250.8 1.5 copy.355
  255.2 1.5 copy.347
  258.1 1.5 copy.338
  263.9 1.5 copy.332
  265.3 1.5 copy.334
  271.1 1.5 copy.328
  274.0 1.5 copy.331
  276.9 3.4 copy.447
  280.4 7.3 %fusion.30 = f32[1,16,8,6,128]{4,2,3,1,0:T(8,128)S(1)} fusion(f32[256,8,6,128]{3,1,2,0:T(8,128)} %all-gather.6.cloned.1.call-done, f32[16,8,6]{1,2,0:T(8,128)S(1)} %copy.368, f32[16,8,6]{1,2,0:T(8,128)S(1)} %copy.367, f32[16,8,6]{1,2,0:T(8,128)S(1)} %copy.365, f32[16,8,6]{1,2,0:T(8,128)S(1)} %copy.364, f32[16,8,6]{1,2,0:T(8,128)S(1)} %copy.362, ...), kind=kLoop, calls=%fused_computation.31 | loop fusion | flops 4423680 | bytes 6776832 | tf_op jit(solution)/shard_map/add | solution.py:91
  287.8 2.4 all_gather.47
  291.7 2.6 multiply_reduce_fusion
  294.9 10.2 %all-to-all-start.2 = ((f32[32,1,16]{2,1,0:T(1,128)}), f32[32,1,16]{2,1,0:T(1,128)S(1)}, u32[]{:S(2)}, u32[]{:S(2)}) async-start(f32[32,1,16]{2,1,0:T(1,128)} %broadcast_in_dim.21), calls=%async_computation.2 | async-start | bytes 32768 | tf_op jit(solution)/shard_map/all_to_all | solution.py:47
  305.2 11.8 %all-to-all-done.2 = f32[32,1,16]{2,1,0:T(1,128)S(1)} async-done(((f32[32,1,16]{2,1,0:T(1,128)}), f32[32,1,16]{2,1,0:T(1,128)S(1)}, u32[]{:S(2)}, u32[]{:S(2)}) %all-to-all-start.2) | async-done | bytes 2080 | tf_op jit(solution)/shard_map/all_to_all | solution.py:47
  317.8 4.8 all-to-all-start.3
  322.6 13.6 %all-to-all-done.3 = f32[32,16,4]{1,2,0:T(4,128)S(1)} async-done(((f32[32,16,4]{1,2,0:T(4,128)}), f32[32,16,4]{1,2,0:T(4,128)S(1)}, u32[]{:S(2)}, u32[]{:S(2)}) %all-to-all-start.3) | async-done | bytes 8224 | tf_op jit(solution)/shard_map/all_to_all | solution.py:47
  337.5 5.1 %all-to-all-start.4 = ((bf16[4,12,192]{2,1,0:T(8,128)(2,1)}), bf16[4,12,192]{2,1,0:T(8,128)(2,1)S(1)}, u32[]{:S(2)}, u32[]{:S(2)}) async-start(bf16[4,12,192]{2,1,0:T(8,128)(2,1)} %convolution_convert_fusion), calls=%async_computation.4 | async-start | bytes 65536 | tf_op jit(solution)/shard_map/all_to_all | solution.py:182
  342.6 4.7 copy.404
  348.1 28.9 %all_gather.52 = bf16[16,48,192]{2,1,0:T(8,128)(2,1)S(1)} all-gather(bf16[1,48,192]{2,1,0:T(8,128)(2,1)S(1)} %all_gather_reshape.3), channel_id=1, replica_groups=mesh['rep'=2,'tp_0'=16,'tp_1'=2,'sub'=4] {'tp_0'}, dimensions={0}, use_global_device_ids=true | all-gather | bytes 313344 | tf_op jit(solution)/shard_map/all_gather | solution.py:63
  377.0 2.4 all-gather.3
  380.6 2.6 reshape.1222
  383.2 2.7 fusion.2
  385.9 5.6 %convolution_bitcast_fusion = f32[32,48,192]{2,1,0:T(8,128)} fusion(bf16[32,192,256]{2,1,0:T(8,128)(2,1)} %bitcast.694, bf16[48,6144]{1,0:T(8,128)(2,1)} %reshape.1222, bf16[1,6144,256]{2,1,0:T(8,128)(2,1)S(1)} %copy-done, f32[48,256]{1,0:T(8,128)S(1)} %fusion.2), kind=kOutput, calls=%fused_computation.4 | convolution fusion | flops 302063616 | bytes 8110080 | tf_op jit(solution)/shard_map/dot_general | solution.py:188
  391.5 83.8 %all_to_all.36 = f32[32,48,192]{2,1,0:T(8,128)} all-to-all(f32[32,48,192]{2,1,0:T(8,128)} %convolution_bitcast_fusion), channel_id=1, replica_groups=mesh['rep'=2,'tp_0'=16,'tp_1'=2,'sub'=4] {'tp_0','tp_1'}, dimensions={0} | all-to-all | bytes 2359296 | tf_op jit(solution)/shard_map/all_to_all | solution.py:82
  475.2 1.5 reduce_sum.69
  476.8 9.4 %all_to_all.37 = bf16[4,12,192]{2,1,0:T(8,128)(2,1)S(1)} all-to-all(bf16[4,12,192]{2,1,0:T(8,128)(2,1)S(1)} %reshape.1223), channel_id=1, replica_groups=mesh['rep'=2,'tp_0'=16,'tp_1'=2,'sub'=4] {'sub'}, dimensions={0} | all-to-all | bytes 36864 | tf_op jit(solution)/shard_map/all_to_all | solution.py:190
  (126 shorter events, 62.2 us)
Async XLA Ops:
  6.5 379.3 %copy-start = (bf16[1,6144,256]{2,1,0:T(8,128)(2,1)S(1)}, bf16[1,6144,256]{2,1,0:T(8,128)(2,1)}, u32[]{:S(2)}) copy-start(bf16[1,6144,256]{2,1,0:T(8,128)(2,1)} %param.26) | copy-start | bytes 9437188
  8.1 66.0 %all-to-all-start = ((bf16[32,16,192]{2,1,0:T(8,128)(2,1)}), bf16[32,16,192]{2,1,0:T(8,128)(2,1)S(1)}, u32[]{:S(2)}, u32[]{:S(2)}) async-start(bf16[32,16,192]{2,1,0:T(8,128)(2,1)} %stack.2), calls=%async_computation | async-start | bytes 524288 | tf_op jit(solution)/shard_map/all_to_all | solution.py:18
  32.9 247.5 %all-gather.6.cloned.1.call-start = ((), (), s32[]{:S(2)}) async-start(), calls=%async_computation.7 | async-start | bytes 6684672 | tf_op jit(solution)/shard_map/all_gather | solution.py:32
  76.5 2.0 copy-start.6
  78.5 0.8 copy-start.1
  81.9 7.4 %copy-start.2 = (bf16[16,1024]{0,1:T(8,128)(2,1)S(1)}, bf16[16,1024]{0,1:T(8,128)(2,1)}, u32[]{:S(2)}) copy-start(bf16[16,1024]{0,1:T(8,128)(2,1)} %get-tuple-element.57) | copy-start | bytes 98308
  84.6 192.3 %all-to-all-start.1 = ((bf16[4,1536,192]{1,2,0:T(8,128)(2,1)}), bf16[4,1536,192]{1,2,0:T(8,128)(2,1)}, u32[]{:S(2)}, u32[]{:S(2)}) async-start(bf16[4,1536,192]{1,2,0:T(8,128)(2,1)} %broadcast_in_dim.20), calls=%async_computation.1 | async-start | bytes 4718592 | tf_op jit(solution)/shard_map/all_to_all | solution.py:47
  154.5 66.9 %copy-start.3 = (f32[16,8,6]{0,1,2:T(8,128)S(1)}, f32[16,8,6]{0,1,2:T(8,128)}, u32[]{:S(2)}) copy-start(f32[16,8,6]{0,1,2:T(8,128)} %copy.411) | copy-start | bytes 9220
  154.5 66.9 %copy-start.4 = (f32[16,8,6]{0,1,2:T(8,128)S(1)}, f32[16,8,6]{0,1,2:T(8,128)}, u32[]{:S(2)}) copy-start(f32[16,8,6]{0,1,2:T(8,128)} %copy.409) | copy-start | bytes 9220
  280.3 9.8 %copy-start.5 = (f32[16,8,128]{2,1,0:T(8,128)S(1)}, f32[16,8,128]{2,1,0:T(8,128)}, u32[]{:S(2)}) copy-start(f32[16,8,128]{2,1,0:T(8,128)} %copy.374) | copy-start | bytes 196612
  280.3 9.8 %copy-start.7 = (f32[16,8,6]{1,2,0:T(8,128)S(1)}, f32[16,8,6]{1,2,0:T(8,128)}, u32[]{:S(2)}) copy-start(f32[16,8,6]{1,2,0:T(8,128)} %copy.371) | copy-start | bytes 9220
  280.3 9.8 %copy-start.8 = (f32[16,8,6]{1,2,0:T(8,128)S(1)}, f32[16,8,6]{1,2,0:T(8,128)}, u32[]{:S(2)}) copy-start(f32[16,8,6]{1,2,0:T(8,128)} %copy.372) | copy-start | bytes 9220
  280.4 9.8 %copy-start.9 = (f32[16,8,6]{1,2,0:T(8,128)S(1)}, f32[16,8,6]{1,2,0:T(8,128)}, u32[]{:S(2)}) copy-start(f32[16,8,6]{1,2,0:T(8,128)} %copy.373) | copy-start | bytes 9220
  280.4 9.8 %copy-start.10 = (f32[16,8,6]{1,2,0:T(8,128)S(1)}, f32[16,8,6]{1,2,0:T(8,128)}, u32[]{:S(2)}) copy-start(f32[16,8,6]{1,2,0:T(8,128)} %copy.393) | copy-start | bytes 9220
  287.7 3.9 copy-start.11
  287.7 17.4 %copy-start.14 = (bf16[192]{0:T(256)(128)(2,1)S(1)}, bf16[192]{0:T(256)(128)(2,1)}, u32[]{:S(2)}) copy-start(bf16[192]{0:T(256)(128)(2,1)} %param.22) | copy-start | bytes 1156
  287.7 29.2 %copy-start.13 = (bf16[192,4]{0,1:T(4,128)(2,1)S(1)}, bf16[192,4]{0,1:T(4,128)(2,1)}, u32[]{:S(2)}) copy-start(bf16[192,4]{0,1:T(4,128)(2,1)} %param.23) | copy-start | bytes 4612
  287.8 34.8 %copy-start.12 = (s32[16,2]{0,1:T(2,128)S(1)}, s32[16,2]{0,1:T(2,128)}, u32[]{:S(2)}) copy-start(s32[16,2]{0,1:T(2,128)} %param.24) | copy-start | bytes 388
  294.9 22.0 %all-to-all-start.2 = ((f32[32,1,16]{2,1,0:T(1,128)}), f32[32,1,16]{2,1,0:T(1,128)S(1)}, u32[]{:S(2)}, u32[]{:S(2)}) async-start(f32[32,1,16]{2,1,0:T(1,128)} %broadcast_in_dim.21), calls=%async_computation.2 | async-start | bytes 32768 | tf_op jit(solution)/shard_map/all_to_all | solution.py:47
  317.8 18.4 %all-to-all-start.3 = ((f32[32,16,4]{1,2,0:T(4,128)}), f32[32,16,4]{1,2,0:T(4,128)S(1)}, u32[]{:S(2)}, u32[]{:S(2)}) async-start(f32[32,16,4]{1,2,0:T(4,128)} %broadcast_in_dim.22), calls=%async_computation.3 | async-start | bytes 131072 | tf_op jit(solution)/shard_map/all_to_all | solution.py:47
  337.5 10.6 %all-to-all-start.4 = ((bf16[4,12,192]{2,1,0:T(8,128)(2,1)}), bf16[4,12,192]{2,1,0:T(8,128)(2,1)S(1)}, u32[]{:S(2)}, u32[]{:S(2)}) async-start(bf16[4,12,192]{2,1,0:T(8,128)(2,1)} %convolution_convert_fusion), calls=%async_computation.4 | async-start | bytes 65536 | tf_op jit(solution)/shard_map/all_to_all | solution.py:182
Sparse Core Ops, SparseCore 0:
  82.0 96.1 all-gather.5
